TPU v7x, 32 devices: a whole 2x2x4 slice. The times are simulated.
32 devices in a mesh: gx: 4 (over y, x), gy: 4 (over z), gz: 2 (over core).
Axes of the slice: x: 2, y: 2, z: 4, core: 2. Of those that a mesh axis runs over, the one named last changes fastest.
Arguments:
- right_side: float32 [5, 512, 8, 128], P(None, ('gx', 'gy', 'gz')), may hold values from -6 to 6
- diag_inverse: bfloat16 [5, 512, 128, 128], P(None, ('gx', 'gy', 'gz')), may hold values from -0.5 to 0.5
- off_blocks: bfloat16 [4, 1024, 128, 128], P(None, ('gx', 'gy', 'gz')), may hold values from -0.375 to 0.375
- live_counts: int32 [5, 32], P(None, ('gx', 'gy', 'gz')), may hold values from 1 to 16, as said below
- source_slot: int32 [4, 1024], P(None, ('gx', 'gy', 'gz')), may hold values from 0 to 15, as said below
- target_owner: int32 [4, 1024], P(None, ('gx', 'gy', 'gz')), may hold values from 0 to 31, as said below
- target_block: int32 [4, 1024], P(None, ('gx', 'gy', 'gz')), may hold values from 16 to 79, as said below
Outputs:
- solution: float32 [5, 512, 8, 128], P(None, ('gx', 'gy', 'gz'))
Inputs may be any that keep to these rules, and one draw needn't show every extreme that they name: `live_counts`: slots at or past a device's count in a level are empty; in every level some device has all 16 slots live. `source_slot`: names a live slot of the issuing device in the same level. `target_owner`: in every level, each device's records go exactly 2 each to 16 distinct owners and none to the others. `target_block`: the level part is later than the record's own level, and the slot is live at the owner in that level.
All inputs are finite; a program needn't handle non-finite values.
Results may differ from a plain program's by a relative error of at most 0.013.
Values sent between devices are 32-bit elements; how exact they have to be, the bound alone decides.
A program may use at most 64 MiB of HBM per device.

v0:
```python
import jax
import jax.numpy as jnp
from jax import lax
from jax.sharding import PartitionSpec as P

CAP = 2


def shards(
    right_side, diag_inverse, off_blocks, live_counts, source_slot, target_owner, target_block
):
    levels_total = right_side.shape[0]
    slots = right_side.shape[1]
    rhs_count = right_side.shape[2]
    width = right_side.shape[3]
    flat_width = rhs_count * width
    records = off_blocks.shape[1]
    owners = lax.axis_size(("gx", "gy", "gz"))
    slot_ids = jnp.arange(slots, dtype=jnp.int32)
    owner_ids = jnp.arange(owners, dtype=jnp.int32)
    buffer_ids = jnp.arange(owners * CAP, dtype=jnp.int32)
    block_ids = jnp.arange(levels_total * slots, dtype=jnp.int32)
    accumulated = jnp.zeros((levels_total * slots, flat_width), jnp.float32)
    results = []
    for level_at in range(levels_total):
        pending = accumulated[level_at * slots : (level_at + 1) * slots].reshape(
            slots, rhs_count, width
        )
        work_rows = (right_side[level_at] - pending).astype(jnp.bfloat16)
        solved = jnp.einsum(
            "srb,sbc->src", work_rows, diag_inverse[level_at], preferred_element_type=jnp.float32
        )
        solved = jnp.where(
            (slot_ids < live_counts[level_at, 0])[:, None, None], solved, jnp.float32(0.0)
        )
        results.append(solved)
        if level_at + 1 < levels_total:
            rounded = solved.astype(jnp.bfloat16)
            picker = (source_slot[level_at][:, None] == slot_ids[None, :]).astype(jnp.bfloat16)
            picked = jnp.einsum(
                "ks,srb->krb", picker, rounded, preferred_element_type=jnp.float32
            ).astype(jnp.bfloat16)
            contribution = jnp.einsum(
                "krb,kbc->krc", picked, off_blocks[level_at], preferred_element_type=jnp.float32
            )
            contribution = contribution.reshape(records, flat_width)
            owners_now = target_owner[level_at]
            blocks_now = target_block[level_at]
            owner_hits = (owners_now[:, None] == owner_ids[None, :]).astype(jnp.int32)
            position = jnp.sum(jnp.cumsum(owner_hits, axis=0) * owner_hits, axis=1) - 1
            slot_of = owners_now * CAP + position
            packer = buffer_ids[:, None] == slot_of[None, :]
            outgoing = jnp.dot(
                packer.astype(jnp.float32), contribution, precision=lax.Precision.HIGHEST
            )
            labels = jnp.sum(packer.astype(jnp.int32) * (blocks_now + 1)[None, :], axis=1) - 1
            arrived, received_labels = (
                lax.all_to_all(
                    outgoing.reshape(owners, CAP, flat_width),
                    ("gx", "gy", "gz"),
                    split_axis=0,
                    concat_axis=0,
                    tiled=True,
                ),
                lax.all_to_all(
                    labels.reshape(owners, CAP),
                    ("gx", "gy", "gz"),
                    split_axis=0,
                    concat_axis=0,
                    tiled=True,
                ),
            )
            arrived = arrived.reshape(owners * CAP, flat_width)
            received_labels = received_labels.reshape(owners * CAP)
            placer = (block_ids[:, None] == received_labels[None, :]).astype(jnp.float32)
            accumulated = accumulated + jnp.dot(placer, arrived, precision=lax.Precision.HIGHEST)
    return jnp.stack(results)


def solution(mesh):
    in_specs = (
        P(None, ("gx", "gy", "gz"), None, None),
        P(None, ("gx", "gy", "gz"), None, None),
        P(None, ("gx", "gy", "gz"), None, None),
        P(None, ("gx", "gy", "gz")),
        P(None, ("gx", "gy", "gz")),
        P(None, ("gx", "gy", "gz")),
        P(None, ("gx", "gy", "gz")),
    )
    out_specs = P(None, ("gx", "gy", "gz"), None, None)
    return jax.shard_map(shards, mesh=mesh, in_specs=in_specs, out_specs=out_specs, check_vma=False)
```

profile of v0, /device:TPU:0, one launch (start us, length us, event | category | flops | bytes accessed | tf_op | source)
XLA Modules:
  0.0 117.0 jit_solution(17567609547212547136)
XLA Ops:
  0.7 1.3 %add_bitcast_fusion = (s32[32]{0:T(128)}, s32[32]{0:T(128)S(1)}, s32[32]{0:T(128)S(1)}, s32[32]{0:T(128)S(1)}) fusion(s32[4,32]{1,0:T(4,128)} %param.13), kind=kLoop, calls=%fused_computation.130 | loop fusion | flops 128 | bytes 1024 | tf_op jit(solution)/shard_map/mul | solution.py:56
  2.3 1.3 %fusion.77 = (s32[32]{0:T(128)}, s32[32]{0:T(128)S(1)}, s32[32]{0:T(128)S(1)}, s32[32]{0:T(128)S(1)}) fusion(s32[32]{0:T(128)S(1)} %select_reduce_fusion.1, s32[4,32]{1,0:T(4,128)} %param.12), kind=kLoop, calls=%fused_computation.122 | loop fusion | flops 96 | bytes 1152 | tf_op jit(solution)/shard_map/eq | solution.py:52
  6.0 7.3 %all-to-all-start = ((s32[32,1,2]{2,1,0:T(1,128)}), s32[32,1,2]{2,1,0:T(1,128)S(1)}, u32[]{:S(2)}, u32[]{:S(2)}) async-start(s32[32,1,2]{2,1,0:T(1,128)} %bitcast.10), calls=%async_computation | async-start | bytes 32768 | tf_op jit(solution)/shard_map/all_to_all | solution.py:65
  13.4 1.4 %slice_bitcast_fusion.3 = (s32[32]{0:T(128)}, s32[32]{0:T(128)S(1)}, s32[32]{0:T(128)S(1)}, s32[32]{0:T(128)}) fusion(s32[4,32]{1,0:T(4,128)} %param.11), kind=kLoop, calls=%fused_computation.129 | loop fusion | bytes 1024 | tf_op jit(solution)/shard_map/eq | solution.py:39
  14.8 1.5 %fusion.81 = (s32[1,1]{0,1:T(1,128)}, s32[1,1]{0,1:T(1,128)}, s32[1,1]{0,1:T(1,128)}, s32[1,1]{0,1:T(1,128)}, s32[1,1]{0,1:T(1,128)}) fusion(s32[5,1]{0,1:T(1,128)} %param.10), kind=kLoop, calls=%fused_computation.150 | loop fusion | bytes 40 | tf_op jit(solution)/shard_map/slice | solution.py:34
  17.0 2.1 %bitcast_dynamic-update-slice_fusion.3 = (f32[5,16,8,128]{3,2,1,0:T(8,128)}, bf16[16,8,128]{2,1,0:T(8,128)(2,1)S(1)}) fusion(bf16[5,16,128,128]{3,2,1,0:T(8,128)(2,1)} %param.8, f32[5,16,8,128]{3,2,1,0:T(8,128)} %param.7, pred[16]{0:T(512)(128)(4,1)S(1)} %iota_compare_fusion.24), kind=kOutput, calls=%fused_computation.52 | convolution fusion | flops 4227071 | bytes 655376 | tf_op jit(solution)/shard_map/srb,sbc->src/dot_general | solution.py:30
  19.3 1.6 %fusion.8 = f32[32,8,128]{2,1,0:T(8,128)S(1)} fusion(bf16[4,32,128,128]{3,2,1,0:T(8,128)(2,1)} %param.9, bf16[32,8,128]{2,0,1:T(8,128)(2,1)S(1)} %convolution_convert_fusion.3), kind=kOutput, calls=%fused_computation.19 | convolution fusion | flops 8388608 | bytes 1245184 | tf_op jit(solution)/shard_map/krb,kbc->krc/dot_general | solution.py:43
  21.3 0.9 copy.31
  22.2 5.8 %all-to-all-start.1 = ((f32[32,2,1024]{2,1,0:T(2,128)}), f32[32,2,1024]{2,1,0:T(2,128)S(1)}, u32[]{:S(2)}, u32[]{:S(2)}) async-start(f32[32,2,1024]{2,1,0:T(2,128)} %copy.31), calls=%async_computation.1 | async-start | bytes 524288 | tf_op jit(solution)/shard_map/all_to_all | solution.py:58
  30.8 7.3 %all-to-all-done.1 = f32[32,2,1024]{2,1,0:T(2,128)S(1)} async-done(((f32[32,2,1024]{2,1,0:T(2,128)}), f32[32,2,1024]{2,1,0:T(2,128)S(1)}, u32[]{:S(2)}, u32[]{:S(2)}) %all-to-all-start.1) | async-done | bytes 262176 | tf_op jit(solution)/shard_map/all_to_all | solution.py:58
  38.0 2.9 %all-to-all-start.2 = ((s32[32,1,2]{2,1,0:T(1,128)}), s32[32,1,2]{2,1,0:T(1,128)S(1)}, u32[]{:S(2)}, u32[]{:S(2)}) async-start(s32[32,1,2]{2,1,0:T(1,128)} %bitcast.22), calls=%async_computation.2 | async-start | bytes 32768 | tf_op jit(solution)/shard_map/all_to_all | solution.py:65
  43.4 1.6 %fusion.6 = f32[32,8,128]{2,1,0:T(8,128)S(1)} fusion(bf16[4,32,128,128]{3,2,1,0:T(8,128)(2,1)} %param.9, bf16[32,8,128]{2,0,1:T(8,128)(2,1)S(1)} %convolution_convert_fusion.2), kind=kOutput, calls=%fused_computation.17 | convolution fusion | flops 8388608 | bytes 1245184 | tf_op jit(solution)/shard_map/krb,kbc->krc/dot_general | solution.py:43
  45.3 0.9 copy.35
  46.2 1.8 %all-to-all-done.2 = s32[32,1,2]{2,1,0:T(1,128)S(1)} async-done(((s32[32,1,2]{2,1,0:T(1,128)}), s32[32,1,2]{2,1,0:T(1,128)S(1)}, u32[]{:S(2)}, u32[]{:S(2)}) %all-to-all-start.2) | async-done | bytes 288 | tf_op jit(solution)/shard_map/all_to_all | solution.py:65
  48.1 4.0 %all-to-all-start.3 = ((f32[32,2,1024]{2,1,0:T(2,128)}), f32[32,2,1024]{2,1,0:T(2,128)S(1)}, u32[]{:S(2)}, u32[]{:S(2)}) async-start(f32[32,2,1024]{2,1,0:T(2,128)} %copy.35), calls=%async_computation.3 | async-start | bytes 524288 | tf_op jit(solution)/shard_map/all_to_all | solution.py:58
  52.9 1.2 %iota_compare_fusion.22 = pred[16]{0:T(512)(128)(4,1)} fusion(s32[]{:T(128)} %bitcast.16), kind=kLoop, calls=%fused_computation.137 | loop fusion | flops 16 | bytes 20 | tf_op jit(solution)/shard_map/lt | solution.py:34
  55.5 6.6 %all-to-all-done.3 = f32[32,2,1024]{2,1,0:T(2,128)S(1)} async-done(((f32[32,2,1024]{2,1,0:T(2,128)}), f32[32,2,1024]{2,1,0:T(2,128)S(1)}, u32[]{:S(2)}, u32[]{:S(2)}) %all-to-all-start.3) | async-done | bytes 262176 | tf_op jit(solution)/shard_map/all_to_all | solution.py:58
  62.1 2.9 %all-to-all-start.4 = ((s32[32,1,2]{2,1,0:T(1,128)}), s32[32,1,2]{2,1,0:T(1,128)S(1)}, u32[]{:S(2)}, u32[]{:S(2)}) async-start(s32[32,1,2]{2,1,0:T(1,128)} %bitcast.34), calls=%async_computation.4 | async-start | bytes 32768 | tf_op jit(solution)/shard_map/all_to_all | solution.py:65
  65.2 1.0 convolution_add_fusion.1
  67.1 1.5 %bitcast_dynamic-update-slice_fusion.1 = (f32[5,16,8,128]{3,2,1,0:T(8,128)}, bf16[16,8,128]{2,1,0:T(8,128)(2,1)S(1)}) fusion(f32[5,16,8,128]{3,2,1,0:T(8,128)} %get-tuple-element.27, bf16[16,8,128]{2,1,0:T(8,128)(2,1)S(1)} %fusion.26, bf16[5,16,128,128]{3,2,1,0:T(8,128)(2,1)S(1)} %copy-done, pred[16]{0:T(512)(128)(4,1)} %iota_compare_fusion.22), kind=kOutput, calls=%fused_computation.50 | convolution fusion | flops 4227072 | bytes 655872 | tf_op jit(solution)/shard_map/srb,sbc->src/dot_general | solution.py:30
  69.4 1.6 %fusion.4 = f32[32,8,128]{2,1,0:T(8,128)S(1)} fusion(bf16[4,32,128,128]{3,2,1,0:T(8,128)(2,1)} %param.9, bf16[32,8,128]{2,0,1:T(8,128)(2,1)S(1)} %convolution_convert_fusion.1), kind=kOutput, calls=%fused_computation.15 | convolution fusion | flops 8388608 | bytes 1245184 | tf_op jit(solution)/shard_map/krb,kbc->krc/dot_general | solution.py:43
  72.2 5.8 %all-to-all-start.5 = ((f32[32,2,1024]{2,1,0:T(2,128)}), f32[32,2,1024]{2,1,0:T(2,128)S(1)}, u32[]{:S(2)}, u32[]{:S(2)}) async-start(f32[32,2,1024]{2,1,0:T(2,128)} %copy.39), calls=%async_computation.5 | async-start | bytes 524288 | tf_op jit(solution)/shard_map/all_to_all | solution.py:58
  78.9 1.1 iota_compare_fusion.21
  81.4 6.7 %all-to-all-done.5 = f32[32,2,1024]{2,1,0:T(2,128)S(1)} async-done(((f32[32,2,1024]{2,1,0:T(2,128)}), f32[32,2,1024]{2,1,0:T(2,128)S(1)}, u32[]{:S(2)}, u32[]{:S(2)}) %all-to-all-start.5) | async-done | bytes 262176 | tf_op jit(solution)/shard_map/all_to_all | solution.py:58
  88.1 2.9 %all-to-all-start.6 = ((s32[32,1,2]{2,1,0:T(1,128)}), s32[32,1,2]{2,1,0:T(1,128)S(1)}, u32[]{:S(2)}, u32[]{:S(2)}) async-start(s32[32,1,2]{2,1,0:T(1,128)} %bitcast.46), calls=%async_computation.6 | async-start | bytes 32768 | tf_op jit(solution)/shard_map/all_to_all | solution.py:65
  91.2 0.9 convolution_add_fusion
  93.0 1.5 %bitcast_dynamic-update-slice_fusion = (f32[5,16,8,128]{3,2,1,0:T(8,128)}, bf16[16,8,128]{2,1,0:T(8,128)(2,1)S(1)}) fusion(f32[5,16,8,128]{3,2,1,0:T(8,128)} %get-tuple-element.29, bf16[16,8,128]{2,1,0:T(8,128)(2,1)S(1)} %fusion.25, bf16[5,16,128,128]{3,2,1,0:T(8,128)(2,1)S(1)} %copy-done, pred[16]{0:T(512)(128)(4,1)} %iota_compare_fusion.21), kind=kOutput, calls=%fused_computation.49 | convolution fusion | flops 4227072 | bytes 655872 | tf_op jit(solution)/shard_map/srb,sbc->src/dot_general | solution.py:30
  95.3 1.6 %fusion.2 = f32[32,8,128]{2,1,0:T(8,128)S(1)} fusion(bf16[4,32,128,128]{3,2,1,0:T(8,128)(2,1)} %param.9, bf16[32,8,128]{2,0,1:T(8,128)(2,1)S(1)} %convolution_convert_fusion), kind=kOutput, calls=%fused_computation.13 | convolution fusion | flops 8388608 | bytes 1245184 | tf_op jit(solution)/shard_map/krb,kbc->krc/dot_general | solution.py:43
  97.0 1.0 fusion.41
  98.0 0.9 copy.43
  98.9 5.8 %all-to-all-start.7 = ((f32[32,2,1024]{2,1,0:T(2,128)}), f32[32,2,1024]{2,1,0:T(2,128)S(1)}, u32[]{:S(2)}, u32[]{:S(2)}) async-start(f32[32,2,1024]{2,1,0:T(2,128)} %copy.43), calls=%async_computation.7 | async-start | bytes 524288 | tf_op jit(solution)/shard_map/all_to_all | solution.py:58
  106.2 8.5 %all-to-all-done.7 = f32[32,2,1024]{2,1,0:T(2,128)S(1)} async-done(((f32[32,2,1024]{2,1,0:T(2,128)}), f32[32,2,1024]{2,1,0:T(2,128)S(1)}, u32[]{:S(2)}, u32[]{:S(2)}) %all-to-all-start.7) | async-done | bytes 262176 | tf_op jit(solution)/shard_map/all_to_all | solution.py:58
  (87 shorter events, 23.2 us)
Async XLA Ops:
  5.2 46.9 %copy-start.4 = (s32[32]{0:T(128)}, s32[32]{0:T(128)S(1)}, u32[]{:S(2)}) copy-start(s32[32]{0:T(128)S(1)} %get-tuple-element.17) | copy-start | bytes 388
  6.0 16.1 %all-to-all-start = ((s32[32,1,2]{2,1,0:T(1,128)}), s32[32,1,2]{2,1,0:T(1,128)S(1)}, u32[]{:S(2)}, u32[]{:S(2)}) async-start(s32[32,1,2]{2,1,0:T(1,128)} %bitcast.10), calls=%async_computation | async-start | bytes 32768 | tf_op jit(solution)/shard_map/all_to_all | solution.py:65
  13.4 31.6 %copy-start.1 = (s32[32,2]{0,1:T(2,128)}, s32[32,2]{0,1:T(2,128)S(1)}, u32[]{:S(2)}) copy-start(s32[32,2]{0,1:T(2,128)S(1)} %multiply_add_fusion) | copy-start | bytes 772
  17.0 25.3 %copy-start = (bf16[5,16,128,128]{3,2,1,0:T(8,128)(2,1)S(1)}, bf16[5,16,128,128]{3,2,1,0:T(8,128)(2,1)}, u32[]{:S(2)}) copy-start(bf16[5,16,128,128]{3,2,1,0:T(8,128)(2,1)} %param.8) | copy-start | bytes 7864324
  22.2 15.8 %all-to-all-start.1 = ((f32[32,2,1024]{2,1,0:T(2,128)}), f32[32,2,1024]{2,1,0:T(2,128)S(1)}, u32[]{:S(2)}, u32[]{:S(2)}) async-start(f32[32,2,1024]{2,1,0:T(2,128)} %copy.31), calls=%async_computation.1 | async-start | bytes 524288 | tf_op jit(solution)/shard_map/all_to_all | solution.py:58
  38.0 10.0 %all-to-all-start.2 = ((s32[32,1,2]{2,1,0:T(1,128)}), s32[32,1,2]{2,1,0:T(1,128)S(1)}, u32[]{:S(2)}, u32[]{:S(2)}) async-start(s32[32,1,2]{2,1,0:T(1,128)} %bitcast.22), calls=%async_computation.2 | async-start | bytes 32768 | tf_op jit(solution)/shard_map/all_to_all | solution.py:65
  48.1 14.0 %all-to-all-start.3 = ((f32[32,2,1024]{2,1,0:T(2,128)}), f32[32,2,1024]{2,1,0:T(2,128)S(1)}, u32[]{:S(2)}, u32[]{:S(2)}) async-start(f32[32,2,1024]{2,1,0:T(2,128)} %copy.35), calls=%async_computation.3 | async-start | bytes 524288 | tf_op jit(solution)/shard_map/all_to_all | solution.py:58
  62.1 10.2 %all-to-all-start.4 = ((s32[32,1,2]{2,1,0:T(1,128)}), s32[32,1,2]{2,1,0:T(1,128)S(1)}, u32[]{:S(2)}, u32[]{:S(2)}) async-start(s32[32,1,2]{2,1,0:T(1,128)} %bitcast.34), calls=%async_computation.4 | async-start | bytes 32768 | tf_op jit(solution)/shard_map/all_to_all | solution.py:65
  66.1 4.9 %copy-start.2 = (s32[32,2]{0,1:T(2,128)S(1)}, s32[32,2]{0,1:T(2,128)}, u32[]{:S(2)}) copy-start(s32[32,2]{0,1:T(2,128)} %copy-done.1) | copy-start | bytes 772
  66.1 4.9 %copy-start.5 = (s32[32]{0:T(128)S(1)}, s32[32]{0:T(128)}, u32[]{:S(2)}) copy-start(s32[32]{0:T(128)} %copy-done.4) | copy-start | bytes 388
  66.2 11.9 %copy-start.3 = (s32[32]{0:T(128)S(1)}, s32[32]{0:T(128)}, u32[]{:S(2)}) copy-start(s32[32]{0:T(128)} %get-tuple-element.9) | copy-start | bytes 388
  66.2 11.9 %copy-start.6 = (s32[32]{0:T(128)S(1)}, s32[32]{0:T(128)}, u32[]{:S(2)}) copy-start(s32[32]{0:T(128)} %get-tuple-element.5) | copy-start | bytes 388
  72.2 15.8 %all-to-all-start.5 = ((f32[32,2,1024]{2,1,0:T(2,128)}), f32[32,2,1024]{2,1,0:T(2,128)S(1)}, u32[]{:S(2)}, u32[]{:S(2)}) async-start(f32[32,2,1024]{2,1,0:T(2,128)} %copy.39), calls=%async_computation.5 | async-start | bytes 524288 | tf_op jit(solution)/shard_map/all_to_all | solution.py:58
  88.1 10.8 %all-to-all-start.6 = ((s32[32,1,2]{2,1,0:T(1,128)}), s32[32,1,2]{2,1,0:T(1,128)S(1)}, u32[]{:S(2)}, u32[]{:S(2)}) async-start(s32[32,1,2]{2,1,0:T(1,128)} %bitcast.46), calls=%async_computation.6 | async-start | bytes 32768 | tf_op jit(solution)/shard_map/all_to_all | solution.py:65
  98.9 15.8 %all-to-all-start.7 = ((f32[32,2,1024]{2,1,0:T(2,128)}), f32[32,2,1024]{2,1,0:T(2,128)S(1)}, u32[]{:S(2)}, u32[]{:S(2)}) async-start(f32[32,2,1024]{2,1,0:T(2,128)} %copy.43), calls=%async_computation.7 | async-start | bytes 524288 | tf_op jit(solution)/shard_map/all_to_all | solution.py:58
where the time goes:
time: 118 us; the launch traced here: 117 us
  starting transfers between devices  37.5 us (32%)
  waiting for transfers between devices  30.9 us (26%)
  matrix products  19.7 us (17%)
  other arithmetic  15.3 us (13%)
  local copies, waits for them, and re-layouts  13.1 us (11%)
    all_to_all x4, waiting for transfers between devices, shards(): lax.all_to_all(outgoing.reshape(owners, CAP, flat_width), ('gx', 'gy', 'g...  29.1 us
    all_to_all x4, starting transfers between devices, shards(): lax.all_to_all(outgoing.reshape(owners, CAP, flat_width), ('gx', 'gy', 'g...  21.5 us
    all_to_all x4, starting transfers between devices, shards(): lax.all_to_all(labels.reshape(owners, CAP), ('gx', 'gy', 'gz'), split_axi...  15.9 us
    dot_general x5, matrix products, shards(): jnp.einsum('srb,sbc->src', work_rows, diag_inverse[level_at], preferred_e...  6.84 us
    dot_general x4, matrix products, shards(): jnp.einsum('krb,kbc->krc', picked, off_blocks[level_at], preferred_elemen...  6.41 us
    lt x5, other arithmetic, shards(): slot_ids < live_counts[level_at, 0]  4.31 us
    dot_general x4, local copies, waits for them, and re-layouts, shards(): jnp.dot(packer.astype(jnp.float32), contribution, precision=lax.Precision...  3.58 us
    convert_element_type x4, other arithmetic, shards(): work_rows = (right_side[level_at] - pending).astype(jnp.bfloat16)  3.41 us
  transfers between devices with their start and end apart: 8, of which 5 were waited for; matrix products, arithmetic and copies ran while one was open for 34% of the time, Pallas kernels for 0%

commit v1 on v0

v1 whole, which is shorter than its diff:
```python
import functools

import jax
import jax.numpy as jnp
from jax import lax
from jax.experimental import pallas as pl
from jax.experimental.pallas import tpu as pltpu
from jax.sharding import PartitionSpec as P

CAP = 2
AXES = ("gx", "gy", "gz")
MESH = pl.DeviceIdType.MESH


def kernel(
    sizes,
    live_ref,
    source_ref,
    record_ref,
    labels_ref,
    right_hbm,
    diag_hbm,
    off_hbm,
    out_hbm,
    work_ref,
    diag_ref,
    off_ref,
    solved_ref,
    made_ref,
    outgoing_ref,
    arrived_ref,
    names_ref,
    load_sem,
    out_sem,
    send_sem,
    recv_sem,
    name_send_sem,
    name_recv_sem,
):
    nx, ny, nz = sizes
    devices = nx * ny * nz
    levels, slots = diag_ref.shape[:2]
    records = off_ref.shape[1]
    rhs = solved_ref.shape[-2]
    pack = CAP * rhs
    level_rows = slots * rhs
    arrivals = devices * CAP
    me = (lax.axis_index("gx") * ny + lax.axis_index("gy")) * nz + lax.axis_index("gz")

    def place(device):
        return (device // (ny * nz), (device // nz) % ny, device % nz)

    def partner(step):
        return lax.rem(me + step, devices)

    right_load = pltpu.make_async_copy(right_hbm, work_ref, load_sem.at[0])
    diag_loads = [
        pltpu.make_async_copy(diag_hbm.at[at], diag_ref.at[at], load_sem.at[1 + at])
        for at in range(levels)
    ]
    off_loads = [
        pltpu.make_async_copy(off_hbm.at[at], off_ref.at[at], load_sem.at[1 + levels + at])
        for at in range(levels - 1)
    ]
    right_load.start()
    for at in range(levels):
        diag_loads[at].start()
        if at < levels - 1:
            off_loads[at].start()

    barrier = pltpu.get_barrier_semaphore()

    @pl.loop(1, devices)
    def _(step):
        pl.semaphore_signal(barrier, inc=1, device_id=place(partner(step)), device_id_type=MESH)

    pl.semaphore_wait(barrier, devices - 1)

    @pl.loop(1, devices)
    def _(step):
        other = partner(step)
        pltpu.make_async_remote_copy(
            src_ref=labels_ref.at[other],
            dst_ref=names_ref.at[me],
            send_sem=name_send_sem,
            recv_sem=name_recv_sem,
            device_id=place(other),
            device_id_type=MESH,
        ).start()

    names_ref[me] = labels_ref[me]
    right_load.wait()

    names = None
    for at in range(levels):
        diag_loads[at].wait()
        count = live_ref[at, 0]
        for slot in range(slots):
            row = (at * slots + slot) * rhs
            work = work_ref[row : row + rhs, :].astype(jnp.bfloat16)
            solved = jnp.dot(work, diag_ref[at, slot], preferred_element_type=jnp.float32)
            solved_ref[at, slot] = jnp.where(slot < count, solved, jnp.float32(0.0))
        pltpu.make_async_copy(solved_ref.at[at], out_hbm.at[at], out_sem.at[at]).start()
        if at == levels - 1:
            break
        off_loads[at].wait()

        def make(record, carry, at=at):
            picked = solved_ref[at, source_ref[at, record]].astype(jnp.bfloat16)
            made_ref[record] = jnp.dot(
                picked, off_ref[at, record], preferred_element_type=jnp.float32
            )
            return carry

        lax.fori_loop(0, records, make, 0, unroll=True)

        def send(step, carry, at=at):
            other = partner(step)
            for copy_at in range(CAP):
                outgoing_ref[at, pl.ds(other * pack + copy_at * rhs, rhs), :] = made_ref[
                    record_ref[at, other * CAP + copy_at]
                ]
            pltpu.make_async_remote_copy(
                src_ref=outgoing_ref.at[at, pl.ds(other * pack, pack)],
                dst_ref=arrived_ref.at[at, pl.ds(me * pack, pack)],
                send_sem=send_sem.at[at],
                recv_sem=recv_sem.at[at],
                device_id=place(other),
                device_id_type=MESH,
            ).start()
            return carry

        lax.fori_loop(1, devices, send, 0)
        for copy_at in range(CAP):
            arrived_ref[at, pl.ds(me * pack + copy_at * rhs, rhs), :] = made_ref[
                record_ref[at, me * CAP + copy_at]
            ]

        if at == 0:
            pltpu.make_async_copy(
                names_ref.at[pl.ds(0, devices - 1)],
                names_ref.at[pl.ds(0, devices - 1)],
                name_recv_sem,
            ).wait()
            names = jnp.sum(names_ref[...], axis=0)

        later_rows = (levels - 1 - at) * slots
        ids = lax.broadcasted_iota(jnp.int32, (later_rows, arrivals), 0) + (
            (at + 1) * slots + 1
        )
        hit = (ids == names[at : at + 1, :arrivals]).astype(jnp.float32).astype(jnp.bfloat16)
        placer = jnp.concatenate([hit, hit], axis=1)

        incoming = arrived_ref.at[at, pl.ds(0, (devices - 1) * pack)]
        pltpu.make_async_copy(incoming, incoming, recv_sem.at[at]).wait()
        for r in range(rhs):
            row = arrived_ref[at, pl.ds(r, arrivals, stride=rhs), :]
            high = row.astype(jnp.bfloat16)
            low = (row - high.astype(jnp.float32)).astype(jnp.bfloat16)
            total = jnp.dot(
                placer,
                jnp.concatenate([high, low], axis=0),
                preferred_element_type=jnp.float32,
            )
            where = pl.ds((at + 1) * level_rows + r, later_rows, stride=rhs)
            work_ref[where, :] = work_ref[where, :] - total

    for at in range(levels):
        pltpu.make_async_copy(solved_ref.at[at], out_hbm.at[at], out_sem.at[at]).wait()
    name_part = labels_ref.at[pl.ds(0, devices - 1)]
    pltpu.make_async_copy(name_part, name_part, name_send_sem).wait()
    for at in range(levels - 1):
        part = outgoing_ref.at[at, pl.ds(0, (devices - 1) * pack)]
        pltpu.make_async_copy(part, part, send_sem.at[at]).wait()


def shards(
    sizes,
    right_side,
    diag_inverse,
    off_blocks,
    live_counts,
    source_slot,
    target_owner,
    target_block,
):
    levels, slots, rhs, width = right_side.shape
    records = off_blocks.shape[1]
    devices = sizes[0] * sizes[1] * sizes[2]
    arrivals = devices * CAP
    lanes = -(-arrivals // 128) * 128
    me = (lax.axis_index("gx") * sizes[1] + lax.axis_index("gy")) * sizes[2] + lax.axis_index(
        "gz"
    )

    record_ids = jnp.arange(records, dtype=jnp.int32)
    same = (target_owner[:, :, None] == target_owner[:, None, :]) & (
        record_ids[None, None, :] < record_ids[None, :, None]
    )
    slot_of = target_owner * CAP + jnp.sum(same.astype(jnp.int32), axis=2)
    packer = slot_of[:, None, :] == jnp.arange(arrivals, dtype=jnp.int32)[None, :, None]
    record_at = jnp.sum(jnp.where(packer, record_ids[None, None, :], 0), axis=2)
    label = jnp.sum(jnp.where(packer, target_block[:, None, :] + 1, 0), axis=2)
    label = label.reshape(levels - 1, devices, CAP).transpose(1, 0, 2)
    lane_ids = jnp.arange(lanes, dtype=jnp.int32)
    labels = jnp.zeros((devices, levels - 1, lanes), jnp.int32)
    for copy_at in range(CAP):
        labels = jnp.where(
            lane_ids[None, None, :] == me * CAP + copy_at, label[:, :, copy_at : copy_at + 1], labels
        )

    smem = pl.BlockSpec(memory_space=pltpu.SMEM)
    vmem = pl.BlockSpec(memory_space=pltpu.VMEM)
    anywhere = pl.BlockSpec(memory_space=pl.ANY)
    return pl.pallas_call(
        functools.partial(kernel, sizes),
        out_shape=jax.ShapeDtypeStruct((levels, slots, rhs, width), jnp.float32),
        in_specs=[smem, smem, smem, vmem, anywhere, anywhere, anywhere],
        out_specs=anywhere,
        scratch_shapes=[
            pltpu.VMEM((levels * slots * rhs, width), jnp.float32),
            pltpu.VMEM(diag_inverse.shape, diag_inverse.dtype),
            pltpu.VMEM(off_blocks.shape, off_blocks.dtype),
            pltpu.VMEM((levels, slots, rhs, width), jnp.float32),
            pltpu.VMEM((records, rhs, width), jnp.float32),
            pltpu.VMEM((levels - 1, arrivals * rhs, width), jnp.float32),
            pltpu.VMEM((levels - 1, arrivals * rhs, width), jnp.float32),
            pltpu.VMEM((devices, levels - 1, lanes), jnp.int32),
            pltpu.SemaphoreType.DMA((2 * levels,)),
            pltpu.SemaphoreType.DMA((levels,)),
            pltpu.SemaphoreType.DMA((levels - 1,)),
            pltpu.SemaphoreType.DMA((levels - 1,)),
            pltpu.SemaphoreType.DMA,
            pltpu.SemaphoreType.DMA,
        ],
        compiler_params=pltpu.CompilerParams(
            collective_id=0, has_side_effects=True, vmem_limit_bytes=60 * 1024 * 1024
        ),
    )(
        live_counts,
        source_slot,
        record_at,
        labels,
        right_side.reshape(levels * slots * rhs, width),
        diag_inverse,
        off_blocks,
    )


def solution(mesh):
    sizes = tuple(mesh.shape[axis] for axis in AXES)
    in_specs = (
        P(None, AXES, None, None),
        P(None, AXES, None, None),
        P(None, AXES, None, None),
        P(None, AXES),
        P(None, AXES),
        P(None, AXES),
        P(None, AXES),
    )
    return jax.shard_map(
        functools.partial(shards, sizes),
        mesh=mesh,
        in_specs=in_specs,
        out_specs=P(None, AXES, None, None),
        check_vma=False,
    )
```

time: 118 us -> 51.1 us (0.43)
  Pallas kernels: 0 us -> 44.5 us
  starting transfers between devices: 37.5 us -> 0 us
  waiting for transfers between devices: 30.9 us -> 0 us
  matrix products: 19.7 us -> 0 us
  other arithmetic: 15.3 us -> 3.16 us
  local copies, waits for them, and re-layouts: 13.1 us -> 3.17 us
    pallas_call x0 -> x1, Pallas kernels: none -> 44.5 us  [shards(): pl.pallas_call(functools.partial(kernel, sizes), out_shape=jax.ShapeDtype...]
    all_to_all x8 -> x0, starting transfers between devices: 37.5 us -> none  [the longest x4 21.5 us: shards(): lax.all_to_all(outgoing.reshape(owners, CAP, flat_width), ('gx', 'gy', 'g...]
    all_to_all x8 -> x0, waiting for transfers between devices: 30.9 us -> none  [the longest x4 29.1 us: shards(): lax.all_to_all(outgoing.reshape(owners, CAP, flat_width), ('gx', 'gy', 'g...]
    dot_general x21 -> x0, matrix products: 19.7 us -> none  [the longest x5 6.84 us: shards(): jnp.einsum('srb,sbc->src', work_rows, diag_inverse[level_at], preferred_e...]
    lt x5 -> x1, other arithmetic: 4.31 us -> 0.01 us  [shards(): record_ids[None, None, :] < record_ids[None, :, None]]
    convert_element_type x8 -> x0, other arithmetic: 3.7 us -> none  [the longest x4 3.41 us: shards(): work_rows = (right_side[level_at] - pending).astype(jnp.bfloat16)]
    eq x6 -> x0, local copies, waits for them, and re-layouts: 3.66 us -> none  [the longest x4 1.55 us: shards(): block_ids[:, None] == received_labels[None, :]]
    dot_general x4 -> x0, local copies, waits for them, and re-layouts: 3.58 us -> none  [shards(): jnp.dot(packer.astype(jnp.float32), contribution, precision=lax.Precision...]
  transfers between devices with their start and end apart: 8 -> 0, of which waited for: 5 -> 0; matrix products, arithmetic and copies ran while one was open for 34% -> 0% of each run, Pallas kernels for 0% -> 0%
where the time goes in v1:
time: 51.1 us; the launch traced here: 50.8 us
  Pallas kernels  44.5 us (87%)
  local copies, waits for them, and re-layouts  3.17 us (6%)
  other arithmetic  3.16 us (6%)
    pallas_call x1, Pallas kernels, shards(): pl.pallas_call(functools.partial(kernel, sizes), out_shape=jax.ShapeDtype...  44.5 us
    unnamed x2, local copies, waits for them, and re-layouts  3.04 us

profile of v1, /device:TPU:0, one launch (start us, length us, event | category | flops | bytes accessed | tf_op | source)
XLA Modules:
  0.0 50.8 jit_solution(6615637045788998475)
XLA Ops:
  0.0 1.3 %copy.21.live_ref = s32[5,1]{1,0:T(8,128)} copy(s32[5,1]{0,1:T(1,128)} %param.10) | data formatting | bytes 40 | tf_op args[3]
  1.3 1.0 %convert_reduce_fusion = s32[4,32]{1,0:T(4,128)S(1)} fusion(s32[4,32]{1,0:T(4,128)} %param.12, pred[32,32]{1,0:T(8,128)(4,1)S(1)} %iota_compare_fusion.1), kind=kLoop, calls=%fused_computation.4 | loop fusion | flops 16256 | bytes 2048 | tf_op jit(solution)/shard_map/reduce_sum | solution.py:200
  2.3 0.7 %multiply_add_fusion = (s32[4,32]{1,0:T(4,128)S(1)}, s32[4,32]{1,0:T(4,128)S(1)}) fusion(s32[4,32]{1,0:T(4,128)S(1)} %convert_reduce_fusion, s32[4,32]{1,0:T(4,128)} %param.12, s32[4,32]{1,0:T(4,128)} %param.13), kind=kLoop, calls=%fused_computation.6 | loop fusion | flops 384 | bytes 2560 | tf_op jit(solution)/shard_map/add | solution.py:200
  3.0 0.7 %select_reduce_fusion = (s32[4,64]{1,0:T(4,128)S(1)}, s32[4,64]{1,0:T(4,128)}) fusion(s32[4,32]{1,0:T(4,128)S(1)} %get-tuple-element.10, s32[4,32]{1,0:T(4,128)S(1)} %get-tuple-element.9), kind=kLoop, calls=%fused_computation.1 | loop fusion | flops 40448 | bytes 3072 | tf_op jit(solution)/shard_map/reduce_sum | solution.py:203
  3.7 0.1 copy.16
  3.9 0.8 %select_select_fusion.labels_ref = s32[32,4,128]{2,1,0:T(4,128)} fusion(s32[32,4]{1,0:T(8,128)S(1)} %bitcast.9, s32[32,4]{1,0:T(8,128)S(1)} %bitcast.8, pred[128]{0:T(512)(128)(4,1)S(1)} %get-tuple-element.11, pred[128]{0:T(512)(128)(4,1)S(1)} %get-tuple-element.12), kind=kLoop, calls=%fused_computation | loop fusion | flops 32768 | bytes 66816 | tf_op jit(solution)/shard_map/jit(_where)/select_n | solution.py:208
  4.6 44.5 %shard_map.73 = f32[5,16,8,128]{3,2,1,0:T(8,128)} custom-call(s32[5,1]{1,0:T(8,128)} %copy.21.live_ref, s32[4,32]{1,0:T(4,128)} %source_ref.1, s32[4,64]{1,0:T(4,128)} %get-tuple-element.6.record_ref, s32[32,4,128]{2,1,0:T(4,128)} %select_select_fusion.labels_ref, f32[640,128]{1,0:T(8,128)} %bitcast.6, bf16[5,16,128,128]{3,2,1,0:T(8,128)(2,1)} %diag_hbm.1, ...), custom_call_target="tpu_custom_call" | custom-call | tf_op jit(solution)/shard_map/pallas_call | solution.py:215
  49.1 1.7 %copy.25 = f32[5,16,8,128]{3,2,1,0:T(8,128)} copy(f32[5,16,8,128]{3,2,1,0:T(8,128)} %shard_map.73) | data formatting | bytes 655360
  (3 shorter events, 0.0 us)

commit v2 on v1

v2 whole, which is shorter than its diff:
```python
import functools

import jax
import jax.numpy as jnp
from jax import lax
from jax.experimental import pallas as pl
from jax.experimental.pallas import tpu as pltpu
from jax.sharding import PartitionSpec as P

CAP = 2
GROUP = 8
AXES = ("gx", "gy", "gz")
MESH = pl.DeviceIdType.MESH


def kernel(
    sizes,
    live_ref,
    source_ref,
    owner_ref,
    block_ref,
    right_hbm,
    diag_hbm,
    off_hbm,
    out_hbm,
    work_ref,
    diag_ref,
    off_refs,
    solved_ref,
    outgoing_ref,
    arrived_ref,
    names_out_ref,
    names_ref,
    record_vmem,
    record_ref,
    load_sem,
    out_sem,
    record_sem,
    send_sem,
    recv_sem,
    name_send_sem,
    name_recv_sem,
):
    nx, ny, nz = sizes
    devices = nx * ny * nz
    plane = nx * nz
    levels, slots = diag_ref.shape[:2]
    records = off_refs[0].shape[0]
    rhs = solved_ref.shape[-2]
    pack = CAP * rhs
    level_rows = slots * rhs
    lanes = names_ref.shape[-1]
    mx, my, mz = (lax.axis_index(axis) for axis in AXES)
    me = (mx * ny + my) * nz + mz

    def partner(index):
        at = index // plane
        down = ny - 1 - at
        down = down - jnp.where(down > my, 0, 1)
        up = at + jnp.where(at < my, 0, 1)
        oy = jnp.where(at == ny - 1, my, jnp.where(2 * my < ny, down, up))
        rest = lax.rem(index, plane) + 1
        ox = lax.rem(mx + rest // nz, nx)
        oz = lax.rem(mz + lax.rem(rest, nz), nz)
        return (ox * ny + oy) * nz + oz, (ox, oy, oz)

    right_load = pltpu.make_async_copy(right_hbm, work_ref, load_sem.at[0])
    diag_loads = [
        pltpu.make_async_copy(diag_hbm.at[at], diag_ref.at[at], load_sem.at[1 + at])
        for at in range(levels)
    ]
    off_loads = [
        pltpu.make_async_copy(off_hbm.at[at], off_refs[at], load_sem.at[1 + levels + at])
        for at in range(levels - 1)
    ]
    barrier = pltpu.get_barrier_semaphore()

    @pl.loop(0, devices - 1)
    def _(index):
        pl.semaphore_signal(barrier, inc=1, device_id=partner(index)[1], device_id_type=MESH)

    right_load.start()
    for at in range(levels):
        diag_loads[at].start()
        if at < levels - 1:
            off_loads[at].start()

    owner_ids = lax.broadcasted_iota(jnp.int32, (devices, records), 0)
    record_ids = lax.broadcasted_iota(jnp.int32, (devices, records), 1)
    lane_ids = lax.broadcasted_iota(jnp.int32, (devices, lanes), 1)
    told = jnp.zeros((devices, lanes), jnp.float32)
    index = jnp.zeros((devices, lanes), jnp.int32)
    for at in range(levels - 1):
        hits = owner_ids == owner_ref[at : at + 1, :]
        block_row = (block_ref[at : at + 1, :] + 1).astype(jnp.float32)
        first = jnp.min(jnp.where(hits, record_ids, records - 1), axis=1, keepdims=True)
        last = jnp.max(jnp.where(hits, record_ids, 0), axis=1, keepdims=True)
        for copy_at, record in enumerate((first, last)):
            chosen = jnp.where(hits & (record_ids == record), block_row, 0.0)
            label = jnp.sum(chosen, axis=1, keepdims=True)
            told = jnp.where(lane_ids == at * CAP + copy_at, label, told)
            index = jnp.where(lane_ids == at * CAP + copy_at, record, index)
    record_vmem[...] = index
    names_out_ref[...] = told.reshape(devices, 1, lanes)
    names_ref[pl.ds(me, 1)] = names_out_ref[pl.ds(me, 1)]
    record_copy = pltpu.make_async_copy(record_vmem, record_ref, record_sem)
    record_copy.start()

    def solve(at):
        diag_loads[at].wait()
        count = live_ref[0, at]
        for slot in range(slots):
            row = (at * slots + slot) * rhs
            work = work_ref[row : row + rhs, :].astype(jnp.bfloat16)
            solved = jnp.dot(work, diag_ref[at, slot], preferred_element_type=jnp.float32)
            solved_ref[at, slot] = jnp.where(slot < count, solved, jnp.float32(0.0))
        pltpu.make_async_copy(solved_ref.at[at], out_hbm.at[at], out_sem.at[at]).start()

    def make(at, other, target_ref, base):
        for copy_at in range(CAP):
            record = record_ref[other, at * CAP + copy_at]
            picked = solved_ref[at, source_ref[at, record]].astype(jnp.bfloat16)
            target_ref[at, pl.ds(base + copy_at * rhs, rhs), :] = jnp.dot(
                picked, off_refs[at][record], preferred_element_type=jnp.float32
            )

    def make_out(at, index):
        other, _ = partner(index)
        make(at, other, outgoing_ref, other * pack)

    def send(at, index):
        other, where = partner(index)
        pltpu.make_async_remote_copy(
            src_ref=outgoing_ref.at[at, pl.ds(other * pack, pack)],
            dst_ref=arrived_ref.at[at, pl.ds(me * pack, pack)],
            send_sem=send_sem.at[at],
            recv_sem=recv_sem.at[at],
            device_id=where,
            device_id_type=MESH,
        ).start()

    def send_all(at):
        groups = devices // GROUP

        @pl.loop(0, groups - 1)
        def _(group):
            for item in range(GROUP):
                make_out(at, group * GROUP + item)
            for item in range(GROUP):
                send(at, group * GROUP + item)

        for index in range(devices - GROUP, devices - 1):
            make_out(at, index)
        for index in range(devices - GROUP, devices - 1):
            send(at, index)
        make(at, me, arrived_ref, me * pack)

    def gather_in(at, names, first, count):
        ids = lax.broadcasted_iota(jnp.int32, (count * slots, devices), 0) + (first * slots + 1)
        hits = [
            (ids == names[at * CAP + copy_at : at * CAP + copy_at + 1, :])
            .astype(jnp.float32)
            .astype(jnp.bfloat16)
            for copy_at in range(CAP)
        ]
        placer = jnp.concatenate(hits + hits, axis=1)
        for r in range(rhs):
            rows = [
                arrived_ref[at, pl.ds(copy_at * rhs + r, devices, stride=pack), :]
                for copy_at in range(CAP)
            ]
            high = [row.astype(jnp.bfloat16) for row in rows]
            low = [
                (row - top.astype(jnp.float32)).astype(jnp.bfloat16)
                for row, top in zip(rows, high)
            ]
            total = jnp.dot(
                placer,
                jnp.concatenate(high + low, axis=0),
                preferred_element_type=jnp.float32,
            )
            where = pl.ds(first * level_rows + r, count * slots, stride=rhs)
            work_ref[where, :] = work_ref[where, :] - total

    right_load.wait()
    solve(0)
    record_copy.wait()
    off_loads[0].wait()
    pl.semaphore_wait(barrier, devices - 1)

    @pl.loop(0, devices - 1)
    def _(index):
        other, where = partner(index)
        pltpu.make_async_remote_copy(
            src_ref=names_out_ref.at[pl.ds(other, 1)],
            dst_ref=names_ref.at[pl.ds(me, 1)],
            send_sem=name_send_sem,
            recv_sem=name_recv_sem,
            device_id=where,
            device_id_type=MESH,
        ).start()

    send_all(0)
    name_part = names_ref.at[pl.ds(0, devices - 1)]
    pltpu.make_async_copy(name_part, name_part, name_recv_sem).wait()
    wanted = -(-(levels - 1) * CAP // 8) * 8
    pick = (
        lax.broadcasted_iota(jnp.int32, (wanted, lanes), 0)
        == lax.broadcasted_iota(jnp.int32, (wanted, lanes), 1)
    ).astype(jnp.float32)
    names = lax.dot_general(
        pick,
        names_ref[...].reshape(devices, lanes),
        (((1,), (1,)), ((), ())),
        preferred_element_type=jnp.float32,
        precision=lax.Precision.HIGHEST,
    ).astype(jnp.int32)

    for at in range(1, levels):
        incoming = arrived_ref.at[at - 1, pl.ds(0, (devices - 1) * pack)]
        pltpu.make_async_copy(incoming, incoming, recv_sem.at[at - 1]).wait()
        gather_in(at - 1, names, at, 1)
        solve(at)
        if at < levels - 1:
            off_loads[at].wait()
            send_all(at)
            gather_in(at - 1, names, at + 1, levels - 1 - at)

    for at in range(levels):
        pltpu.make_async_copy(solved_ref.at[at], out_hbm.at[at], out_sem.at[at]).wait()
    name_part = names_out_ref.at[pl.ds(0, devices - 1)]
    pltpu.make_async_copy(name_part, name_part, name_send_sem).wait()
    for at in range(levels - 1):
        part = outgoing_ref.at[at, pl.ds(0, (devices - 1) * pack)]
        pltpu.make_async_copy(part, part, send_sem.at[at]).wait()


def shards(
    sizes,
    right_side,
    diag_inverse,
    off_blocks,
    live_counts,
    source_slot,
    target_owner,
    target_block,
):
    levels, slots, rhs, width = right_side.shape
    records = off_blocks.shape[1]
    devices = sizes[0] * sizes[1] * sizes[2]
    arrivals = devices * CAP
    lanes = 128
    smem = pl.BlockSpec(memory_space=pltpu.SMEM)
    vmem = pl.BlockSpec(memory_space=pltpu.VMEM)
    anywhere = pl.BlockSpec(memory_space=pl.ANY)
    return pl.pallas_call(
        functools.partial(kernel, sizes),
        out_shape=jax.ShapeDtypeStruct((levels, slots, rhs, width), jnp.float32),
        in_specs=[smem, smem, vmem, vmem, anywhere, anywhere, anywhere],
        out_specs=anywhere,
        scratch_shapes=[
            pltpu.VMEM((levels * slots * rhs, width), jnp.float32),
            pltpu.VMEM(diag_inverse.shape, diag_inverse.dtype),
            tuple(
                pltpu.VMEM(off_blocks.shape[1:], off_blocks.dtype) for _ in range(levels - 1)
            ),
            pltpu.VMEM((levels, slots, rhs, width), jnp.float32),
            pltpu.VMEM((levels - 1, arrivals * rhs, width), jnp.float32),
            pltpu.VMEM((levels - 1, arrivals * rhs, width), jnp.float32),
            pltpu.VMEM((devices, 1, lanes), jnp.float32),
            pltpu.VMEM((devices, 1, lanes), jnp.float32),
            pltpu.VMEM((devices, lanes), jnp.int32),
            pltpu.SMEM((devices, lanes), jnp.int32),
            pltpu.SemaphoreType.DMA((2 * levels,)),
            pltpu.SemaphoreType.DMA((levels,)),
            pltpu.SemaphoreType.DMA,
            pltpu.SemaphoreType.DMA((levels - 1,)),
            pltpu.SemaphoreType.DMA((levels - 1,)),
            pltpu.SemaphoreType.DMA,
            pltpu.SemaphoreType.DMA,
        ],
        compiler_params=pltpu.CompilerParams(
            collective_id=0, has_side_effects=True, vmem_limit_bytes=60 * 1024 * 1024
        ),
    )(
        live_counts.reshape(1, levels),
        source_slot,
        target_owner,
        target_block,
        right_side.reshape(levels * slots * rhs, width),
        diag_inverse,
        off_blocks,
    )


def solution(mesh):
    sizes = tuple(mesh.shape[axis] for axis in AXES)
    in_specs = (
        P(None, AXES, None, None),
        P(None, AXES, None, None),
        P(None, AXES, None, None),
        P(None, AXES),
        P(None, AXES),
        P(None, AXES),
        P(None, AXES),
    )
    return jax.shard_map(
        functools.partial(shards, sizes),
        mesh=mesh,
        in_specs=in_specs,
        out_specs=P(None, AXES, None, None),
        check_vma=False,
    )
```

time: 51.1 us -> 44 us (0.86)
  other arithmetic: 3.16 us -> 0 us
  Pallas kernels: 44.5 us -> 42.1 us
  local copies, waits for them, and re-layouts: 3.17 us -> 1.72 us
    pallas_call x1, Pallas kernels: 44.5 us -> 42.1 us  [shards(): pl.pallas_call(functools.partial(kernel, sizes), out_shape=jax.ShapeDtype...]
    reduce_sum x2 -> x0, other arithmetic: 1.67 us -> none  [the longest x1 0.97 us: shards(): slot_of = target_owner * CAP + jnp.sum(same.astype(jnp.int32), axis=2)]
    unnamed x2 -> x1, local copies, waits for them, and re-layouts: 3.04 us -> 1.72 us
    select_n x1 -> x0, other arithmetic: 0.77 us -> none  [shards(): jnp.where(lane_ids[None, None, :] == me * CAP + copy_at, label[:, :, copy...]
    add x1 -> x0, other arithmetic: 0.71 us -> none  [shards(): slot_of = target_owner * CAP + jnp.sum(same.astype(jnp.int32), axis=2)]
where the time goes in v2:
time: 44 us; the launch traced here: 43.9 us
  Pallas kernels  42.1 us (96%)
  local copies, waits for them, and re-layouts  1.72 us (4%)
    pallas_call x1, Pallas kernels, shards(): pl.pallas_call(functools.partial(kernel, sizes), out_shape=jax.ShapeDtype...  42.1 us
    unnamed x1, local copies, waits for them, and re-layouts  1.72 us

profile of v2, /device:TPU:0, one launch (start us, length us, event | category | flops | bytes accessed | tf_op | source)
XLA Modules:
  0.0 43.9 jit_solution(414098174018846579)
XLA Ops:
  0.0 42.1 %shard_map.73 = f32[5,16,8,128]{3,2,1,0:T(8,128)} custom-call(s32[1,5]{1,0:T(1,128)} %bitcast.3, s32[4,32]{1,0:T(4,128)} %source_ref.1, s32[4,32]{1,0:T(4,128)} %owner_ref.1, s32[4,32]{1,0:T(4,128)} %block_ref.1, f32[640,128]{1,0:T(8,128)} %bitcast.2, bf16[5,16,128,128]{3,2,1,0:T(8,128)(2,1)} %diag_hbm.1, bf16[4,32,128,128]{3,2,1,0:T(8,128)(2,1)} %off_hbm.1), custom_call_target="tpu_custom_call" | custom-call | tf_op jit(solution)/shard_map/pallas_call | solution.py:256
  42.2 1.7 %copy.9 = f32[5,16,8,128]{3,2,1,0:T(8,128)} copy(f32[5,16,8,128]{3,2,1,0:T(8,128)} %shard_map.73) | data formatting | bytes 655360

commit v3 on v2

--- a/solution.py
+++ b/solution.py
@@ -8,7 +8,7 @@
 from jax.sharding import PartitionSpec as P
 
 CAP = 2
-GROUP = 8
+GROUP = 4
 AXES = ("gx", "gy", "gz")
 MESH = pl.DeviceIdType.MESH
 

time: 44 us -> 43.6 us (level)
  no operation moved by 1% of the time
where the time goes in v3:
time: 43.6 us; the launch traced here: 43.5 us
  Pallas kernels  41.7 us (96%)
  local copies, waits for them, and re-layouts  1.72 us (4%)
    pallas_call x1, Pallas kernels, shards(): pl.pallas_call(functools.partial(kernel, sizes), out_shape=jax.ShapeDtype...  41.7 us
    unnamed x1, local copies, waits for them, and re-layouts  1.72 us

profile of v3, /device:TPU:0, one launch (start us, length us, event | category | flops | bytes accessed | tf_op | source)
XLA Modules:
  0.0 43.5 jit_solution(12261662498209413027)
XLA Ops:
  0.0 41.7 %shard_map.73 = f32[5,16,8,128]{3,2,1,0:T(8,128)} custom-call(s32[1,5]{1,0:T(1,128)} %bitcast.3, s32[4,32]{1,0:T(4,128)} %source_ref.1, s32[4,32]{1,0:T(4,128)} %owner_ref.1, s32[4,32]{1,0:T(4,128)} %block_ref.1, f32[640,128]{1,0:T(8,128)} %bitcast.2, bf16[5,16,128,128]{3,2,1,0:T(8,128)(2,1)} %diag_hbm.1, bf16[4,32,128,128]{3,2,1,0:T(8,128)(2,1)} %off_hbm.1), custom_call_target="tpu_custom_call" | custom-call | tf_op jit(solution)/shard_map/pallas_call | solution.py:256
  41.8 1.7 %copy.9 = f32[5,16,8,128]{3,2,1,0:T(8,128)} copy(f32[5,16,8,128]{3,2,1,0:T(8,128)} %shard_map.73) | data formatting | bytes 655360
